TPU v7x, 256 devices: a whole 4x4x8 slice. The times are simulated.
256 devices in a mesh: pipe: 2 (over core), dp: 64 (over y, x_hi, z), mp: 2 (over x_lo).
Axes of the slice: x: 4 (x_hi: 2, x_lo: 2; x = x_hi * 2 + x_lo), y: 4, z: 8, core: 2. Of those that a mesh axis runs over, the one named last changes fastest.
Arguments:
- token_ids: int32 [2, 32768], P('pipe', 'dp'), may hold values from 0 to 32127, as said below
- embedded: bfloat16 [2, 32768, 4096], P('pipe', 'dp', 'mp'), may hold values from -720 to 720
- norm_gain: float32 [2, 4096], P('pipe', 'mp'), may hold values from 0.25 to 1.75
- proj_grad: bfloat16 [2, 32768, 2048], P('pipe', 'dp'), may hold values from -6 to 6
- proj_weight: bfloat16 [2, 4096, 2048], P('pipe', 'mp'), may hold values from -0.125 to 0.125
- stream_grad: bfloat16 [2, 32768, 4096], P('pipe', 'dp', 'mp'), may hold values from -6 to 6
Outputs:
- table_grad: float32 [32128, 2, 2048], P('dp', 'mp', 'pipe')
Inputs may be any that keep to these rules, and one draw needn't show every extreme that they name: `token_ids`: call block o the ids o * 502 to (o + 1) * 502 - 1. The 512 tokens of one stack on one index of dp hold at most 16 ids of any one block, and some block gets exactly 16 of them.
All inputs are finite; a program needn't handle non-finite values.
Results may differ from a plain program's by a relative error of at most 0.0029.
Values may be sent and summed in bfloat16 or wider, within the bound.
A program may use at most 128 MiB of HBM per device.

v0:
```python
import jax
import jax.numpy as jnp
from jax import lax
from jax.sharding import PartitionSpec as P

D = 4096
VOCAB = 32128


epsilon = 1e-06


def sent_to_all(shard, axis):
    copies = jnp.broadcast_to(shard, (lax.axis_size(axis), *shard.shape))
    return lax.all_to_all(copies, axis, split_axis=0, concat_axis=0, tiled=True)


def taken_together(shard, axis):
    everything = sent_to_all(shard, axis)
    return jnp.sum(everything, axis=0)


def packed_total(arrays, axis):
    ends = [0]
    for a in arrays:
        ends.append(ends[-1] + a.size)
    total = taken_together(jnp.concatenate([a.ravel() for a in arrays]), axis)
    return tuple((total[b:e].reshape(a.shape) for a, b, e in zip(arrays, ends, ends[1:])))


def split_up(shard, dim, peers):
    before, after = (shard.shape[:dim], shard.shape[dim + 1 :])
    return jnp.moveaxis(shard.reshape(*before, peers, -1, *after), dim, 0)


def sum_at_owner(shard, axis, dim):
    peers = lax.axis_size(axis)
    blocks = lax.all_to_all(split_up(shard, dim, peers), axis, 0, 0, tiled=True)
    return jnp.sum(blocks, axis=0)


def accumulate(got_rows, got_index, block_rows):
    width = got_rows.shape[-1]
    flat_rows = got_rows.reshape(-1, width)
    flat_index = got_index.reshape(-1)
    selector = (flat_index[None, :] == jnp.arange(block_rows, dtype=jnp.int32)[:, None]).astype(
        jnp.bfloat16
    )
    return jnp.dot(selector, flat_rows, preferred_element_type=jnp.float32)


def on_device(token_ids, embedded, norm_gain, proj_grad, proj_weight, stream_grad):
    projected = lax.dot_general(
        proj_grad[0], proj_weight[0], (((1,), (1,)), ((), ())), preferred_element_type=jnp.float32
    )
    inputs = embedded[0].astype(jnp.float32)
    scaled = projected * norm_gain[0][None, :]
    square_sum, mixed_sum = packed_total(
        (jnp.sum(inputs * inputs, axis=1), jnp.sum(inputs * scaled, axis=1)), "mp"
    )
    inverse = lax.rsqrt(square_sum / D + epsilon)
    norm_back = (
        inverse[:, None] * scaled - inputs * (inverse * inverse * inverse * mixed_sum / D)[:, None]
    )
    grad_rows = (stream_grad[0].astype(jnp.float32) + norm_back).astype(jnp.bfloat16)
    replicas = lax.axis_size("dp")
    tokens_here = grad_rows.shape[0]
    capacity = max(2, 2 * tokens_here // replicas)
    block_rows = VOCAB // replicas
    token_row = token_ids[0]
    owners = token_row // block_rows
    local_row = token_row % block_rows
    matches = (owners[:, None] == jnp.arange(replicas, dtype=jnp.int32)[None, :]).astype(jnp.int32)
    earlier = jnp.cumsum(matches, axis=0) - matches
    position = owners * capacity + jnp.sum(earlier * matches, axis=1)
    placer = (
        position[None, :] == jnp.arange(replicas * capacity, dtype=jnp.int32)[:, None]
    ).astype(jnp.bfloat16)
    send_rows = jnp.dot(placer, grad_rows, preferred_element_type=jnp.float32).astype(jnp.bfloat16)
    send_rows = send_rows.reshape(replicas, capacity, grad_rows.shape[1])
    send_index = jnp.full((replicas * capacity,), block_rows, jnp.int32).at[position].set(local_row)
    send_index = send_index.reshape(replicas, capacity)
    got_rows, got_index = (
        lax.all_to_all(send_rows, "dp", split_axis=0, concat_axis=0, tiled=True),
        lax.all_to_all(send_index, "dp", split_axis=0, concat_axis=0, tiled=True),
    )
    partial_table = accumulate(got_rows, got_index, block_rows)
    half_table = sum_at_owner(partial_table, "pipe", 1)
    return half_table.reshape(block_rows, 1, half_table.shape[1])


def solution(mesh):
    return jax.shard_map(
        on_device,
        mesh=mesh,
        in_specs=(
            P("pipe", "dp"),
            P("pipe", "dp", "mp"),
            P("pipe", "mp"),
            P("pipe", "dp", None),
            P("pipe", "mp", None),
            P("pipe", "dp", "mp"),
        ),
        out_specs=P("dp", "mp", "pipe"),
        check_vma=False,
    )
```

profile of v0, /device:TPU:1, one launch (start us, length us, event | category | flops | bytes accessed | tf_op | source)
XLA Modules:
  0.0 182.2 jit_solution(13732305055713075326)
XLA Ops:
  0.0 0.0 copy-start
  0.0 1.6 copy-done
  1.6 0.0 copy-start.1
  1.6 0.0 copy-start.2
  1.6 10.0 %fusion.2 = (f32[512]{0:T(512)S(1)}, f32[512]{0:T(512)S(1)}, f32[512,2048]{1,0:T(8,128)}) fusion(bf16[1,512,2048]{2,1,0:T(8,128)(2,1)} %param.7, f32[2048]{0:T(1024)} %bitcast.87, bf16[1,2048,2048]{2,1,0:T(8,128)(2,1)} %param.10, bf16[1,512,2048]{2,1,0:T(8,128)(2,1)S(1)} %copy-done), kind=kOutput, calls=%fused_computation.6 | convolution fusion | flops 4301257728 | bytes 16789504 | tf_op jit(solution)/shard_map/dot_general | solution.py:53
  11.6 0.6 broadcast_in_dim.5
  12.2 3.3 %all-to-all-start.1 = ((f32[2,1,1024]{2,1,0:T(1,128)}), f32[2,1,1024]{2,1,0:T(1,128)S(1)}, u32[]{:S(2)}, u32[]{:S(2)}) async-start(f32[2,1,1024]{2,1,0:T(1,128)} %broadcast_in_dim.5), calls=%async_computation.1 | async-start | bytes 16384 | tf_op jit(solution)/shard_map/all_to_all | solution.py:15
  15.5 0.0 copy-done.1
  15.6 1.2 reduce-window.6
  16.8 0.2 slice_reduce_fusion
  17.1 0.1 fusion.20
  17.2 2.4 %scatter_custom_fusion = s32[1024]{0:T(1024)S(1)} fusion(s32[512]{0:T(512)S(1)} %bitcast.86, s32[512]{0:T(512)S(1)} %get-tuple-element.11, s32[]{:T(128)} %constant.30.clone.1), kind=kCustom, calls=%fused_computation.50 | custom fusion | bytes 4100 | tf_op jit(solution)/shard_map/scatter | solution.py:81
  19.7 0.7 all_to_all.16
  20.4 0.0 all-to-all-done.1
  20.4 15.0 %all-to-all-start = ((s32[64,1,16]{2,1,0:T(1,128)}), s32[64,1,16]{2,1,0:T(1,128)S(1)}, u32[]{:S(2)}, u32[]{:S(2)}) async-start(s32[64,1,16]{2,1,0:T(1,128)} %bitcast.8), calls=%async_computation | async-start | bytes 65536 | tf_op jit(solution)/shard_map/all_to_all | solution.py:85
  35.5 0.0 copy-done.2
  35.5 8.2 %convolution_convert_fusion = bf16[1024,2048]{1,0:T(8,128)(2,1)} fusion(f32[512,2048]{1,0:T(8,128)} %get-tuple-element.15, bf16[1,512,2048]{2,1,0:T(8,128)(2,1)} %param.11, bf16[1,512,2048]{2,1,0:T(8,128)(2,1)} %param.7, f32[512]{0:T(512)S(1)} %get-tuple-element.10, f32[512]{0:T(512)S(1)} %get-tuple-element.9, f32[2048]{0:T(1024)S(1)} %bitcast.88, ...), kind=kOutput, calls=%fused_computation.11 | convolution fusion | flops 2158493696 | bytes 12597248 | tf_op jit(solution)/shard_map/dot_general | solution.py:79
  43.6 2.5 %all-to-all-done = s32[64,1,16]{2,1,0:T(1,128)S(1)} async-done(((s32[64,1,16]{2,1,0:T(1,128)}), s32[64,1,16]{2,1,0:T(1,128)S(1)}, u32[]{:S(2)}, u32[]{:S(2)}) %all-to-all-start) | async-done | bytes 4128 | tf_op jit(solution)/shard_map/all_to_all | solution.py:85
  46.1 10.0 %all-to-all-start.2 = ((bf16[64,16,2048]{2,1,0:T(8,128)(2,1)}), bf16[64,16,2048]{2,1,0:T(8,128)(2,1)}, u32[]{:S(2)}, u32[]{:S(2)}) async-start(bf16[64,16,2048]{2,1,0:T(8,128)(2,1)} %bitcast.78), calls=%async_computation.2 | async-start | bytes 8388608 | tf_op jit(solution)/shard_map/all_to_all | solution.py:84
  56.1 0.5 broadcast.143
  56.6 0.7 reduce.10
  57.4 0.1 eq.59
  57.4 91.3 %all-to-all-done.2 = bf16[64,16,2048]{2,1,0:T(8,128)(2,1)} async-done(((bf16[64,16,2048]{2,1,0:T(8,128)(2,1)}), bf16[64,16,2048]{2,1,0:T(8,128)(2,1)}, u32[]{:S(2)}, u32[]{:S(2)}) %all-to-all-start.2) | async-done | bytes 4194336 | tf_op jit(solution)/shard_map/all_to_all | solution.py:84
  148.8 6.4 %copy.19 = bf16[1024,2048]{0,1:T(8,128)(2,1)} copy(bf16[1024,2048]{1,0:T(8,128)(2,1)} %bitcast.19) | data formatting | bytes 8388608 | tf_op jit(solution)/shard_map/reshape | solution.py:44
  155.2 4.5 %convolution_bitcast_fusion = f32[2,502,1024]{2,1,0:T(8,128)S(1)} fusion(bf16[2,1024,1024]{2,1,0:T(8,128)(2,1)} %bitcast.79, s32[1024]{0:T(1024)S(1)} %eq.59), kind=kOutput, calls=%fused_computation.12 | convolution fusion | flops 2106054656 | bytes 8310784 | tf_op jit(solution)/shard_map/dot_general | solution.py:49
  159.7 14.1 %all_to_all.25 = f32[2,502,1024]{2,1,0:T(8,128)} all-to-all(f32[2,502,1024]{2,1,0:T(8,128)S(1)} %convolution_bitcast_fusion), channel_id=1, replica_groups=mesh['pipe'=2,'dp'=64,'mp'=2] {'pipe'}, dimensions={0} | all-to-all | bytes 8224768 | tf_op jit(solution)/shard_map/all_to_all | solution.py:38
  173.8 4.1 %reduce_sum.55 = f32[502,1024]{1,0:T(8,128)} reduce(f32[2,502,1024]{2,1,0:T(8,128)} %all_to_all.25, f32[]{:T(128)} %constant.36.clone.1), dimensions={0}, to_apply=%region_7.8 | reduce | flops 514048 | bytes 6168580 | tf_op jit(solution)/shard_map/reduce_sum | solution.py:39
  177.9 4.3 %reshape.146 = f32[502,1,1024]{2,1,0:T(1,128)} reshape(f32[502,1024]{1,0:T(8,128)} %reduce_sum.55) | data formatting | bytes 4112384 | tf_op jit(solution)/shard_map/reshape | solution.py:89
  (12 shorter events, 0.2 us)
Async XLA Ops:
  0.0 1.6 copy-start
  1.6 13.9 %copy-start.1 = (s32[1,512]{1,0:T(1,128)S(1)}, s32[1,512]{1,0:T(1,128)}, u32[]{:S(2)}) copy-start(s32[1,512]{1,0:T(1,128)} %param.6) | copy-start | bytes 6148
  1.6 33.9 %copy-start.2 = (f32[1,2048]{1,0:T(1,128)S(1)}, f32[1,2048]{1,0:T(1,128)}, u32[]{:S(2)}) copy-start(f32[1,2048]{1,0:T(1,128)} %param.8) | copy-start | bytes 24580
  12.2 8.2 %all-to-all-start.1 = ((f32[2,1,1024]{2,1,0:T(1,128)}), f32[2,1,1024]{2,1,0:T(1,128)S(1)}, u32[]{:S(2)}, u32[]{:S(2)}) async-start(f32[2,1,1024]{2,1,0:T(1,128)} %broadcast_in_dim.5), calls=%async_computation.1 | async-start | bytes 16384 | tf_op jit(solution)/shard_map/all_to_all | solution.py:15
  20.4 25.8 %all-to-all-start = ((s32[64,1,16]{2,1,0:T(1,128)}), s32[64,1,16]{2,1,0:T(1,128)S(1)}, u32[]{:S(2)}, u32[]{:S(2)}) async-start(s32[64,1,16]{2,1,0:T(1,128)} %bitcast.8), calls=%async_computation | async-start | bytes 65536 | tf_op jit(solution)/shard_map/all_to_all | solution.py:85
  46.1 102.6 %all-to-all-start.2 = ((bf16[64,16,2048]{2,1,0:T(8,128)(2,1)}), bf16[64,16,2048]{2,1,0:T(8,128)(2,1)}, u32[]{:S(2)}, u32[]{:S(2)}) async-start(bf16[64,16,2048]{2,1,0:T(8,128)(2,1)} %bitcast.78), calls=%async_computation.2 | async-start | bytes 8388608 | tf_op jit(solution)/shard_map/all_to_all | solution.py:84
where the time goes:
time: 183 us; the launch traced here: 182 us
  waiting for transfers between devices  93.8 us (51%)
  starting transfers between devices  28.3 us (15%)
  matrix products  22.6 us (12%)
  local copies, waits for them, and re-layouts  16.9 us (9%)
  blocking collectives  14.1 us (8%)
  other arithmetic  6.31 us (3%)
    all_to_all x1, waiting for transfers between devices, on_device(): lax.all_to_all(send_rows, 'dp', split_axis=0, concat_axis=0, tiled=True)  91.3 us
    all_to_all x1, starting transfers between devices, on_device(): lax.all_to_all(send_index, 'dp', split_axis=0, concat_axis=0, tiled=True)  15 us
    all_to_all x1, blocking collectives, sum_at_owner(): blocks = lax.all_to_all(split_up(shard, dim, peers), axis, 0, 0, tiled=True)  14.1 us
    dot_general x1, matrix products, on_device(): lax.dot_general(proj_grad[0], proj_weight[0], (((1,), (1,)), ((), ())), p...  9.98 us
    all_to_all x1, starting transfers between devices, on_device(): lax.all_to_all(send_rows, 'dp', split_axis=0, concat_axis=0, tiled=True)  9.96 us
    dot_general x1, matrix products, on_device(): jnp.dot(placer, grad_rows, preferred_element_type=jnp.float32)  8.15 us
    reshape x1, local copies, waits for them, and re-layouts, accumulate(): flat_rows = got_rows.reshape(-1, width)  6.41 us
    dot_general x1, matrix products, accumulate(): return jnp.dot(selector, flat_rows, preferred_element_type=jnp.float32)  4.52 us
  transfers between devices with their start and end apart: 3, of which 2 were waited for; matrix products, arithmetic and copies ran while one was open for 7% of the time, Pallas kernels for 0%

commit v1 on v0

v1 whole, which is shorter than its diff:
```python
import jax
import jax.numpy as jnp
from jax import lax
from jax.experimental import pallas as pl
from jax.experimental.pallas import tpu as pltpu
from jax.sharding import PartitionSpec as P

D = 4096
VOCAB = 32128
EPS = 1e-06

TOK = 512
CAP = 16
VR = 502
VP = 512
NDP = 64
INNER = 2048
FEAT = 2048
CF = 256
NB = FEAT // CF
NC = NB // 2
SLOTS = NDP * CAP
HALF = VR // 2
MESH = pl.DeviceIdType.MESH
NT = (((1,), (1,)), ((), ()))
F32 = jnp.float32
BF16 = jnp.bfloat16
I32 = jnp.int32


def placement(ids):
    block = lax.broadcasted_iota(I32, (NDP, TOK), 0)
    low = block * VR
    inside = jnp.logical_and(ids >= low, ids < low + VR)
    match = jnp.where(inside, 1.0, 0.0)
    before = jnp.where(
        lax.broadcasted_iota(I32, (TOK, TOK), 0) < lax.broadcasted_iota(I32, (TOK, TOK), 1), 1.0, 0.0
    ).astype(BF16)
    earlier = jnp.dot(match.astype(BF16), before, preferred_element_type=F32)
    slot = jnp.sum(match * (earlier + (block * CAP).astype(F32)), axis=0, keepdims=True).astype(I32)
    row = jnp.sum(match * (ids - low - HALF).astype(F32), axis=0, keepdims=True)
    placer = jnp.where(lax.broadcasted_iota(I32, (SLOTS, TOK), 0) == slot, 1.0, 0.0).astype(BF16)
    rows = lax.dot_general(
        placer, jnp.broadcast_to(row, (128, TOK)).astype(BF16), NT, preferred_element_type=F32
    )
    return placer, rows.astype(BF16).reshape(NDP, CAP, 128)


def kernel(
    ids_ref,
    gain_ref,
    emb_hbm,
    pg_hbm,
    w_hbm,
    st_hbm,
    out_hbm,
    pg,
    w,
    emb,
    st,
    scaled,
    square,
    mixed,
    inv,
    coef,
    sums_tx,
    sums_rx,
    ids_rx,
    place,
    rows_tx,
    rows_rx,
    send,
    recv,
    isend,
    irecv,
    onehot,
    table,
    in_sem,
    sum_sem,
    ids_sem,
    row_ssem,
    row_rsem,
    ssem,
    rsem,
    issem,
    irsem,
    osem,
):
    core = lax.axis_index("pipe")
    me = lax.axis_index("dp")
    half = lax.axis_index("mp")
    y, x, z = me // 16, (me // 8) % 2, me % 8

    def peer(q, k, dz):
        spot = (q + k) % 8
        return ((y + spot // 2) % 4) * 16 + ((x + spot) % 2) * 8 + (z + dz) % 8

    def to_peers(act):
        def step(q, carry):
            for k, dz in enumerate((0, 4, 3, 5, 2, 6, 1, 7)):
                if dz == 0:
                    @pl.when(q > 0)
                    def _():
                        act(peer(q, k, dz))
                else:
                    act(peer(q, k, dz))
            return carry

        lax.fori_loop(0, 8, step, 0)

    barrier = pltpu.get_barrier_semaphore()
    to_peers(lambda t: pl.semaphore_signal(barrier, inc=1, device_id={"dp": t}, device_id_type=MESH))
    pl.semaphore_signal(barrier, inc=1, device_id={"mp": 1 - half}, device_id_type=MESH)
    pl.semaphore_signal(barrier, inc=1, device_id={"pipe": 1 - core}, device_id_type=MESH)

    pg_in = pltpu.make_async_copy(pg_hbm.at[0], pg, in_sem.at[0])
    pg_in.start()

    def w_in(b):
        return pltpu.make_async_copy(w_hbm.at[0, pl.ds(b * CF, CF), :], w.at[b], in_sem.at[1 + b])

    def emb_in(b):
        return pltpu.make_async_copy(
            emb_hbm.at[0, :, pl.ds(b * CF, CF)], emb.at[b], in_sem.at[1 + NB + b]
        )

    def st_in(b):
        return pltpu.make_async_copy(
            st_hbm.at[0, :, pl.ds(b * CF, CF)], st.at[b], in_sem.at[1 + 2 * NB + b]
        )

    for b in range(NB):
        w_in(b).start()
        emb_in(b).start()
    for b in range(NB):
        st_in(b).start()

    placer, rows = placement(ids_ref[...])
    place[0] = placer
    isend[:, 0:CAP, :] = rows
    square[...] = jnp.zeros_like(square)
    mixed[...] = jnp.zeros_like(mixed)
    pg_in.wait()

    def project(b, carry):
        pltpu.make_async_copy(w_hbm.at[0, pl.ds(0, CF), :], w.at[b], in_sem.at[1 + b]).wait()
        pltpu.make_async_copy(
            emb_hbm.at[0, :, pl.ds(0, CF)], emb.at[b], in_sem.at[1 + NB + b]
        ).wait()
        s = lax.dot_general(pg[...], w[b], NT, preferred_element_type=F32) * gain_ref[b]
        scaled[b] = s
        e = emb[b].astype(F32)
        ee, es = e * e, e * s
        square[...] += ee[:, :128] + ee[:, 128:]
        mixed[...] += es[:, :128] + es[:, 128:]
        return carry

    lax.fori_loop(0, NB, project, 0)

    sums_tx[0:1] = jnp.sum(square[...].T, axis=0, keepdims=True)
    sums_tx[1:2] = jnp.sum(mixed[...].T, axis=0, keepdims=True)
    for b in range(NB):
        st_in(b).wait()
    pl.semaphore_wait(barrier, NDP - 1 + 2)

    sums_copy = pltpu.make_async_remote_copy(
        src_ref=sums_tx,
        dst_ref=sums_rx,
        send_sem=sum_sem.at[0],
        recv_sem=sum_sem.at[1],
        device_id={"mp": 1 - half},
        device_id_type=MESH,
    )
    ids_copy = pltpu.make_async_remote_copy(
        src_ref=ids_ref,
        dst_ref=ids_rx,
        send_sem=ids_sem.at[0],
        recv_sem=ids_sem.at[1],
        device_id={"pipe": 1 - core},
        device_id_type=MESH,
    )
    ids_copy.start()
    sums_copy.start()

    ids_copy.wait()
    placer, rows = placement(ids_rx[...])
    place[1] = placer
    isend[:, CAP : 2 * CAP, :] = rows

    sums_copy.wait()
    total = sums_tx[...] + sums_rx[...]
    inverse = lax.rsqrt(total[0:1] / D + EPS)
    factor = inverse * inverse * inverse * total[1:2] / D
    inv[...] = jnp.broadcast_to(inverse, (128, TOK)).T
    coef[...] = jnp.broadcast_to(factor, (128, TOK)).T

    def finished(b):
        def lanes(i):
            cut = slice(i * 128, (i + 1) * 128)
            back = inv[...] * scaled[b, :, cut] - emb[b, :, cut].astype(F32) * coef[...]
            return (st[b, :, cut].astype(F32) + back).astype(BF16)

        return jnp.concatenate([lanes(i) for i in range(CF // 128)], axis=1)

    def swap(c):
        return pltpu.make_async_remote_copy(
            src_ref=rows_tx.at[c],
            dst_ref=rows_rx.at[c],
            send_sem=row_ssem.at[c],
            recv_sem=row_rsem.at[c],
            device_id={"pipe": 1 - core},
            device_id_type=MESH,
        )

    def out_copy(src, dst, s, r, t):
        return pltpu.make_async_remote_copy(
            src_ref=src.at[t],
            dst_ref=dst.at[me],
            send_sem=s,
            recv_sem=r,
            device_id={"dp": t},
            device_id_type=MESH,
        )

    to_peers(lambda t: out_copy(isend, irecv, issem, irsem, t).start())
    irecv[me] = isend[me]

    for c in range(NC):
        rows_tx[c] = finished((1 - core) * NC + c)
        swap(c).start()
        send[c, :, 0:CAP, :] = (
            jnp.dot(place[0], finished(core * NC + c), preferred_element_type=F32)
            .astype(BF16)
            .reshape(NDP, CAP, CF)
        )
        swap(c).wait()
        send[c, :, CAP : 2 * CAP, :] = (
            jnp.dot(place[1], rows_rx[c], preferred_element_type=F32)
            .astype(BF16)
            .reshape(NDP, CAP, CF)
        )
        recv[c, me] = send[c, me]
        to_peers(lambda t: out_copy(send.at[c], recv.at[c], ssem.at[c], rsem.at[c], t).start())

    def all_but_one(ref, sem):
        part = ref.at[pl.ds(0, NDP - 1)]
        pltpu.make_async_copy(part, part, sem).wait()

    all_but_one(irecv, irsem)
    index = irecv[...].astype(F32).reshape(2 * SLOTS, 128).T[0:1].astype(I32) + HALF
    onehot[...] = jnp.where(lax.broadcasted_iota(I32, (VP, 2 * SLOTS), 0) == index, 1.0, 0.0).astype(BF16)

    def put(c):
        return pltpu.make_async_copy(
            table.at[c], out_hbm.at[:, pl.ds(c * CF, CF)], osem.at[c]
        )

    for c in range(NC):
        all_but_one(recv.at[c], rsem.at[c])
        sums = jnp.dot(
            onehot[...], recv[c].reshape(2 * SLOTS, CF), preferred_element_type=F32
        )
        table[c] = sums[:VR]
        put(c).start()
    all_but_one(isend, issem)
    for c in range(NC):
        all_but_one(send.at[c], ssem.at[c])
        put(c).wait()


def on_device(token_ids, embedded, norm_gain, proj_grad, proj_weight, stream_grad):
    anywhere = pl.BlockSpec(memory_space=pl.ANY)
    vmem = pl.BlockSpec(memory_space=pltpu.VMEM)
    dma = pltpu.SemaphoreType.DMA
    table = pl.pallas_call(
        kernel,
        out_shape=jax.ShapeDtypeStruct((VR, FEAT // 2), F32),
        in_specs=[vmem, vmem] + [anywhere] * 4,
        out_specs=anywhere,
        scratch_shapes=[
            pltpu.VMEM((TOK, INNER), BF16),
            pltpu.VMEM((NB, CF, INNER), BF16),
            pltpu.VMEM((NB, TOK, CF), BF16),
            pltpu.VMEM((NB, TOK, CF), BF16),
            pltpu.VMEM((NB, TOK, CF), F32),
            pltpu.VMEM((TOK, 128), F32),
            pltpu.VMEM((TOK, 128), F32),
            pltpu.VMEM((TOK, 128), F32),
            pltpu.VMEM((TOK, 128), F32),
            pltpu.VMEM((2, TOK), F32),
            pltpu.VMEM((2, TOK), F32),
            pltpu.VMEM((1, TOK), I32),
            pltpu.VMEM((2, SLOTS, TOK), BF16),
            pltpu.VMEM((NC, TOK, CF), BF16),
            pltpu.VMEM((NC, TOK, CF), BF16),
            pltpu.VMEM((NC, NDP, 2 * CAP, CF), BF16),
            pltpu.VMEM((NC, NDP, 2 * CAP, CF), BF16),
            pltpu.VMEM((NDP, 2 * CAP, 128), BF16),
            pltpu.VMEM((NDP, 2 * CAP, 128), BF16),
            pltpu.VMEM((VP, 2 * SLOTS), BF16),
            pltpu.VMEM((NC, VR, CF), F32),
            dma((1 + 3 * NB,)),
            dma((2,)),
            dma((2,)),
            dma((NC,)),
            dma((NC,)),
            dma((NC,)),
            dma((NC,)),
            dma,
            dma,
            dma((NC,)),
        ],
        compiler_params=pltpu.CompilerParams(
            collective_id=0, has_side_effects=True, vmem_limit_bytes=58 * 1024 * 1024
        ),
    )(
        token_ids,
        norm_gain.reshape(NB, 1, CF),
        embedded,
        proj_grad,
        proj_weight,
        stream_grad,
    )
    return table.reshape(VR, 1, FEAT // 2)


def solution(mesh):
    return jax.shard_map(
        on_device,
        mesh=mesh,
        in_specs=(
            P("pipe", "dp"),
            P("pipe", "dp", "mp"),
            P("pipe", "mp"),
            P("pipe", "dp", None),
            P("pipe", "mp", None),
            P("pipe", "dp", "mp"),
        ),
        out_specs=P("dp", "mp", "pipe"),
        check_vma=False,
    )
```

time: 183 us -> 132 us (0.72)
  Pallas kernels: 0 us -> 127 us
  waiting for transfers between devices: 93.8 us -> 0 us
  starting transfers between devices: 28.3 us -> 0 us
  matrix products: 22.6 us -> 0 us
  blocking collectives: 14.1 us -> 0 us
  local copies, waits for them, and re-layouts: 16.9 us -> 5 us
  other arithmetic: 6.31 us -> 0 us
    pallas_call x0 -> x1, Pallas kernels: none -> 127 us  [on_device(): pl.pallas_call(kernel, out_shape=jax.ShapeDtypeStruct((VR, FEAT // 2), F3...]
    all_to_all x3 -> x0, waiting for transfers between devices: 93.8 us -> none  [the longest x1 91.3 us: on_device(): lax.all_to_all(send_rows, 'dp', split_axis=0, concat_axis=0, tiled=True)]
    all_to_all x3 -> x0, starting transfers between devices: 28.3 us -> none  [the longest x1 15 us: on_device(): lax.all_to_all(send_index, 'dp', split_axis=0, concat_axis=0, tiled=True)]
    dot_general x3 -> x0, matrix products: 22.6 us -> none  [the longest x1 9.98 us: on_device(): lax.dot_general(proj_grad[0], proj_weight[0], (((1,), (1,)), ((), ())), p...]
    all_to_all x1 -> x0, blocking collectives: 14.1 us -> none  [sum_at_owner(): blocks = lax.all_to_all(split_up(shard, dim, peers), axis, 0, 0, tiled=True)]
    reshape x2 -> x1, local copies, waits for them, and re-layouts: 10.7 us -> 5 us  [on_device(): return table.reshape(VR, 1, FEAT // 2)]
    reduce_sum x3 -> x0, other arithmetic: 4.22 us -> none  [the longest x1 4.08 us: sum_at_owner(): return jnp.sum(blocks, axis=0)]
    scatter x1 -> x0, local copies, waits for them, and re-layouts: 2.45 us -> none  [on_device(): jnp.full((replicas * capacity,), block_rows, jnp.int32).at[position]]
  transfers between devices with their start and end apart: 3 -> 0, of which waited for: 2 -> 0; matrix products, arithmetic and copies ran while one was open for 7% -> 0% of each run, Pallas kernels for 0% -> 0%
where the time goes in v1:
time: 132 us
  Pallas kernels  127 us (96%)
  local copies, waits for them, and re-layouts  5 us (4%)
    pallas_call x1, Pallas kernels, on_device(): pl.pallas_call(kernel, out_shape=jax.ShapeDtypeStruct((VR, FEAT // 2), F3...  127 us
    reshape x1, local copies, waits for them, and re-layouts, on_device(): return table.reshape(VR, 1, FEAT // 2)  5 us

profile of v1, /device:TPU:1, one launch (start us, length us, event | category | flops | bytes accessed | tf_op | source)
XLA Modules:
  0.0 131.9 jit_solution(278319274654429488)
XLA Ops:
  0.0 126.9 %shard_map.64 = f32[502,1024]{1,0:T(8,128)} custom-call(s32[1,512]{1,0:T(1,128)} %ids_ref.1, f32[8,1,256]{2,1,0:T(1,128)} %bitcast.3, bf16[1,512,2048]{2,1,0:T(8,128)(2,1)} %emb_hbm.1, bf16[1,512,2048]{2,1,0:T(8,128)(2,1)} %pg_hbm.1, bf16[1,2048,2048]{2,1,0:T(8,128)(2,1)} %w_hbm.1, bf16[1,512,2048]{2,1,0:T(8,128)(2,1)} %st_hbm.1), custom_call_target="tpu_custom_call" | custom-call | tf_op jit(solution)/shard_map/pallas_call | solution.py:275
  126.9 5.0 %copy.7 = f32[502,1,1024]{2,1,0:T(1,128)} copy(f32[502,1,1024]{2,0,1:T(8,128)} %bitcast.2) | data formatting | bytes 4112384 | tf_op jit(solution)/shard_map/reshape | solution.py:324

commit v2 on v1

v2 whole, which is shorter than its diff:
```python
import jax
import jax.numpy as jnp
from jax import lax
from jax.experimental import pallas as pl
from jax.experimental.pallas import tpu as pltpu
from jax.sharding import PartitionSpec as P

D = 4096
VOCAB = 32128
EPS = 1e-06

TOK = 512
CAP = 16
VR = 502
VP = 504
NDP = 64
INNER = 2048
FEAT = 2048
CF = 128
BF = 256
NB = FEAT // BF
NF = FEAT // CF
NC = NF // 2
SLOTS = NDP * CAP
ROWS = 2 * SLOTS
HALF = VR // 2
GROUP = 8 * 2 * CAP
MOVES = (2, 1, 0, 0, 0, 0, -1, -2)
REMOTE = NDP - 4
MESH = pl.DeviceIdType.MESH
NT = (((1,), (1,)), ((), ()))
F32 = jnp.float32
BF16 = jnp.bfloat16
I32 = jnp.int32


def placement(ids, first):
    block = lax.broadcasted_iota(I32, (NDP, TOK), 0)
    low = block * VR
    inside = jnp.logical_and(ids >= low, ids < low + VR)
    match = jnp.where(inside, 1.0, 0.0)
    before = jnp.where(
        lax.broadcasted_iota(I32, (TOK, TOK), 0) < lax.broadcasted_iota(I32, (TOK, TOK), 1), 1.0, 0.0
    ).astype(BF16)
    earlier = match * jnp.dot(match.astype(BF16), before, preferred_element_type=F32)
    rank = jnp.sum(earlier, axis=0, keepdims=True).astype(I32)
    slot = jnp.sum(earlier + match * (block * CAP).astype(F32), axis=0, keepdims=True).astype(I32)
    placer = jnp.where(lax.broadcasted_iota(I32, (SLOTS, TOK), 0) == slot, 1.0, 0.0).astype(BF16)
    ranks = jnp.where(lax.broadcasted_iota(I32, (128, TOK), 0) == rank + first, 1.0, 0.0).astype(BF16)
    rows = (match * (ids - low - HALF).astype(F32)).astype(BF16)
    return placer, lax.dot_general(rows, ranks, NT, preferred_element_type=F32)


def kernel(
    ids_ref,
    gain_ref,
    emb_hbm,
    pg_hbm,
    w_hbm,
    st_hbm,
    out_hbm,
    pg,
    w,
    emb,
    st,
    scaled,
    square,
    mixed,
    inv,
    coef,
    sums_tx,
    sums_rx,
    ids_rx,
    place,
    rows_tx,
    rows_rx,
    send,
    recv,
    isend,
    irecv,
    onehot,
    far_tx,
    far_rx,
    near_tx,
    near_rx,
    back_tx,
    back_rx,
    table,
    in_sem,
    sum_sem,
    ids_sem,
    row_ssem,
    row_rsem,
    ssem,
    rsem,
    issem,
    irsem,
    tab_ssem,
    tab_rsem,
    osem,
):
    core = lax.axis_index("pipe")
    me = lax.axis_index("dp")
    half = lax.axis_index("mp")
    y, x, z = me // 16, (me // 8) % 2, me % 8
    here = me // 8

    def column(spot):
        return ((y + spot // 2) % 4) * 16 + ((x + spot) % 2) * 8

    def plane(dz):
        return (z + dz + 8) % 8

    def signal(where):
        pl.semaphore_signal(barrier, inc=1, device_id=where, device_id_type=MESH)

    barrier = pltpu.get_barrier_semaphore()
    signal({"mp": 1 - half})
    signal({"pipe": 1 - core})

    def greet(spot, carry):
        for dz in (-2, -1, 1, 2):
            signal({"dp": column(spot) + plane(dz)})

        @pl.when(spot > 0)
        def _():
            signal({"dp": column(spot) + z})

        return carry

    lax.fori_loop(0, 8, greet, 0)

    def in_copy(src, dst, i):
        return pltpu.make_async_copy(src, dst, in_sem.at[i])

    def w_in(b):
        return in_copy(w_hbm.at[0, pl.ds(b * BF, BF), :], w.at[b], 1 + b)

    def emb_in(f):
        return in_copy(emb_hbm.at[0, :, pl.ds(f * CF, CF)], emb.at[f], 1 + NB + f)

    def st_in(f):
        return in_copy(st_hbm.at[0, :, pl.ds(f * CF, CF)], st.at[f], 1 + NB + NF + f)

    pg_in = in_copy(pg_hbm.at[0], pg, 0)
    pg_in.start()
    for b in range(NB):
        w_in(b).start()
        emb_in(2 * b).start()
        emb_in(2 * b + 1).start()
    for f in range(NF):
        st_in(f).start()

    place[0], own_rows = placement(ids_ref[...], 0)
    square[...] = jnp.zeros_like(square)
    mixed[...] = jnp.zeros_like(mixed)

    ids_copy = pltpu.make_async_remote_copy(
        src_ref=ids_ref,
        dst_ref=ids_rx,
        send_sem=ids_sem.at[0],
        recv_sem=ids_sem.at[1],
        device_id={"pipe": 1 - core},
        device_id_type=MESH,
    )
    pl.semaphore_wait(barrier, 41)
    ids_copy.start()
    pg_in.wait()

    def project(b, carry):
        in_copy(w_hbm.at[0, pl.ds(0, BF), :], w.at[b], 1 + b).wait()
        s = lax.dot_general(pg[...], w[b], NT, preferred_element_type=F32) * gain_ref[b]
        for i in range(2):
            f = 2 * b + i
            in_copy(emb_hbm.at[0, :, pl.ds(0, CF)], emb.at[f], 1 + NB + f).wait()
            part = s[:, i * CF : (i + 1) * CF]
            scaled[f] = part
            e = emb[f].astype(F32)
            square[...] += e * e
            mixed[...] += e * part
        return carry

    lax.fori_loop(0, NB, project, 0)

    sums_tx[0:1] = jnp.sum(square[...].T, axis=0, keepdims=True)
    sums_tx[1:2] = jnp.sum(mixed[...].T, axis=0, keepdims=True)

    sums_copy = pltpu.make_async_remote_copy(
        src_ref=sums_tx,
        dst_ref=sums_rx,
        send_sem=sum_sem.at[0],
        recv_sem=sum_sem.at[1],
        device_id={"mp": 1 - half},
        device_id_type=MESH,
    )
    ids_copy.wait()
    sums_copy.start()
    place[1], other_rows = placement(ids_rx[...], CAP)
    isend[...] = (own_rows + other_rows).reshape(NDP, 1, 128)
    for f in range(NF):
        st_in(f).wait()

    def send_blocks(src, dst, s_sem, r_sem, s):
        def step(q, carry):
            for i in (0, 7, 2, 1, 6, 3, 5, 4):
                spot = (q + i) % 8
                owner = column(spot) + plane(s * (4 - i))

                def start(spot=spot, owner=owner, i=i):
                    pltpu.make_async_remote_copy(
                        src_ref=src.at[owner],
                        dst_ref=dst.at[i * 8 + here],
                        send_sem=s_sem,
                        recv_sem=r_sem,
                        device_id={"dp": column(spot) + plane(s * MOVES[i])},
                        device_id_type=MESH,
                    ).start()

                if MOVES[i] == 0:
                    pl.when(spot != 0)(start)
                else:
                    start()
            return carry

        lax.fori_loop(0, 8, step, 0)
        for i in range(8):
            if MOVES[i] == 0:
                dst[i * 8 + here] = src[here * 8 + plane(s * (4 - i))]

    def await_blocks(ref, sem):
        part = ref.at[pl.ds(0, REMOTE)]
        pltpu.make_async_copy(part, part, sem).wait()

    for kind in range(2):
        send_blocks(isend, irecv.at[kind], issem.at[kind], irsem.at[kind], 1 - 2 * kind)

    sums_copy.wait()
    total = sums_tx[...] + sums_rx[...]
    inverse = lax.rsqrt(total[0:1] / D + EPS)
    factor = inverse * inverse * inverse * total[1:2] / D
    inv[...] = jnp.broadcast_to(inverse, (128, TOK)).T
    coef[...] = jnp.broadcast_to(factor, (128, TOK)).T

    def finished(f):
        back = inv[...] * scaled[f] - emb[f].astype(F32) * coef[...]
        return (st[f].astype(F32) + back).astype(BF16)

    def swap(c):
        return pltpu.make_async_remote_copy(
            src_ref=rows_tx.at[c],
            dst_ref=rows_rx.at[c],
            send_sem=row_ssem.at[c],
            recv_sem=row_rsem.at[c],
            device_id={"pipe": 1 - core},
            device_id_type=MESH,
        )

    def hand_over(c):
        rows_tx[c] = finished((1 - core) * NC + c)
        swap(c).start()

    def direction(c):
        return 1 - 2 * (c % 2)

    def spread(c):
        def slots(i, rows):
            send[c, :, i * CAP : (i + 1) * CAP, :] = (
                jnp.dot(place[i], rows, preferred_element_type=F32).astype(BF16).reshape(NDP, CAP, CF)
            )

        slots(0, finished(core * NC + c))
        swap(c).wait()
        slots(1, rows_rx[c])
        send_blocks(send.at[c], recv.at[c], ssem.at[c], rsem.at[c], direction(c))

    def summed(c, first, groups):
        rows = recv[c, first * 8 : (first + groups) * 8].reshape(groups * GROUP, CF)
        picks = onehot[c % 2, :, first * GROUP : (first + groups) * GROUP]
        return jnp.dot(picks, rows, preferred_element_type=F32)

    def pass_on(src, dst, c, i, s):
        return pltpu.make_async_remote_copy(
            src_ref=src.at[c],
            dst_ref=dst.at[c],
            send_sem=tab_ssem.at[i, c],
            recv_sem=tab_rsem.at[i, c],
            device_id={"dp": here * 8 + plane(s)},
            device_id_type=MESH,
        )

    def far(c):
        return pass_on(far_tx, far_rx, c, 0, direction(c))

    def near(c):
        return pass_on(near_tx, near_rx, c, 1, direction(c))

    def back(c):
        return pass_on(back_tx, back_rx, c, 2, -direction(c))

    def put(c):
        return pltpu.make_async_copy(table.at[c], out_hbm.at[:, :, pl.ds(c * CF, CF)], osem.at[c])

    def first_sums(c):
        await_blocks(recv.at[c], rsem.at[c])
        far_tx[c] = summed(c, 0, 3).astype(BF16)
        far(c).start()
        back_tx[c] = summed(c, 5, 3).astype(BF16)
        back(c).start()

    def second_sums(c):
        own = summed(c, 3, 1)
        far(c).wait()
        near_tx[c] = (own + far_rx[c].astype(F32)).astype(BF16)
        near(c).start()

    def last_sums(c):
        own = summed(c, 4, 1)
        back(c).wait()
        own = own + back_rx[c].astype(F32)
        near(c).wait()
        own = own + near_rx[c].astype(F32)
        table[c] = own[:VR].reshape(VR, 1, CF)
        put(c).start()

    AHEAD = 2
    for c in range(AHEAD):
        hand_over(c)
    for c in range(AHEAD):
        spread(c)

    slot = lax.broadcasted_iota(I32, (NDP, ROWS), 1)
    unfold = jnp.where(slot // (2 * CAP) == lax.broadcasted_iota(I32, (NDP, ROWS), 0), 1.0, 0.0).astype(BF16)
    lane = lax.broadcasted_iota(I32, (2 * CAP, ROWS), 1) % (2 * CAP)
    take = lane == lax.broadcasted_iota(I32, (2 * CAP, ROWS), 0)
    for kind in range(2):
        await_blocks(irecv.at[kind], irsem.at[kind])
        got = irecv[kind].reshape(NDP, 128).T[: 2 * CAP].astype(BF16)
        spots = jnp.dot(got, unfold, preferred_element_type=F32)
        index = jnp.sum(jnp.where(take, spots, 0.0), axis=0, keepdims=True).astype(I32) + HALF
        onehot[kind] = jnp.where(lax.broadcasted_iota(I32, (VP, ROWS), 0) == index, 1.0, 0.0).astype(BF16)

    for c in range(NC + 2):
        if c + AHEAD < NC:
            hand_over(c + AHEAD)
        if c < NC:
            first_sums(c)
        if c + AHEAD < NC:
            spread(c + AHEAD)
        if 0 <= c - 1 < NC:
            second_sums(c - 1)
        if 0 <= c - 2 < NC:
            last_sums(c - 2)

    for kind in range(2):
        await_blocks(isend, issem.at[kind])
    for c in range(NC):
        await_blocks(send.at[c], ssem.at[c])
        put(c).wait()


def on_device(token_ids, embedded, norm_gain, proj_grad, proj_weight, stream_grad):
    anywhere = pl.BlockSpec(memory_space=pl.ANY)
    vmem = pl.BlockSpec(memory_space=pltpu.VMEM)
    dma = pltpu.SemaphoreType.DMA
    return pl.pallas_call(
        kernel,
        out_shape=jax.ShapeDtypeStruct((VR, 1, FEAT // 2), F32),
        in_specs=[vmem, vmem] + [anywhere] * 4,
        out_specs=anywhere,
        scratch_shapes=[
            pltpu.VMEM((TOK, INNER), BF16),
            pltpu.VMEM((NB, BF, INNER), BF16),
            pltpu.VMEM((NF, TOK, CF), BF16),
            pltpu.VMEM((NF, TOK, CF), BF16),
            pltpu.VMEM((NF, TOK, CF), F32),
            pltpu.VMEM((TOK, 128), F32),
            pltpu.VMEM((TOK, 128), F32),
            pltpu.VMEM((TOK, 128), F32),
            pltpu.VMEM((TOK, 128), F32),
            pltpu.VMEM((2, TOK), F32),
            pltpu.VMEM((2, TOK), F32),
            pltpu.VMEM((1, TOK), I32),
            pltpu.VMEM((2, SLOTS, TOK), BF16),
            pltpu.VMEM((NC, TOK, CF), BF16),
            pltpu.VMEM((NC, TOK, CF), BF16),
            pltpu.VMEM((NC, NDP, 2 * CAP, CF), BF16),
            pltpu.VMEM((NC, NDP, 2 * CAP, CF), BF16),
            pltpu.VMEM((NDP, 1, 128), F32),
            pltpu.VMEM((2, NDP, 1, 128), F32),
            pltpu.VMEM((2, VP, ROWS), BF16),
            pltpu.VMEM((NC, VP, CF), BF16),
            pltpu.VMEM((NC, VP, CF), BF16),
            pltpu.VMEM((NC, VP, CF), BF16),
            pltpu.VMEM((NC, VP, CF), BF16),
            pltpu.VMEM((NC, VP, CF), BF16),
            pltpu.VMEM((NC, VP, CF), BF16),
            pltpu.VMEM((NC, VR, 1, CF), F32),
            dma((1 + NB + 2 * NF,)),
            dma((2,)),
            dma((2,)),
            dma((NC,)),
            dma((NC,)),
            dma((NC,)),
            dma((NC,)),
            dma((2,)),
            dma((2,)),
            dma((3, NC)),
            dma((3, NC)),
            dma((NC,)),
        ],
        compiler_params=pltpu.CompilerParams(
            collective_id=0, has_side_effects=True, vmem_limit_bytes=58 * 1024 * 1024
        ),
    )(
        token_ids,
        norm_gain.reshape(NB, 1, BF),
        embedded,
        proj_grad,
        proj_weight,
        stream_grad,
    )


def solution(mesh):
    return jax.shard_map(
        on_device,
        mesh=mesh,
        in_specs=(
            P("pipe", "dp"),
            P("pipe", "dp", "mp"),
            P("pipe", "mp"),
            P("pipe", "dp", None),
            P("pipe", "mp", None),
            P("pipe", "dp", "mp"),
        ),
        out_specs=P("dp", "mp", "pipe"),
        check_vma=False,
    )
```

time: 132 us -> 106 us (0.80); the launches traced: 132 us -> 103 us
  Pallas kernels: 127 us -> 99.2 us
    pallas_call x1, Pallas kernels: 127 us -> 99.2 us  [on_device(): pl.pallas_call(kernel, out_shape=jax.ShapeDtypeStruct((VR, 1, FEAT // 2),...]
    reshape x1 -> x0, local copies, waits for them, and re-layouts: 5 us -> none  [on_device(): return table.reshape(VR, 1, FEAT // 2)]
    unnamed x0 -> x1, local copies, waits for them, and re-layouts: none -> 4.29 us
where the time goes in v2:
time: 106 us; the launch traced here: 103 us
  Pallas kernels  99.2 us (94%)
  local copies, waits for them, and re-layouts  4.29 us (4%)
    pallas_call x1, Pallas kernels, on_device(): pl.pallas_call(kernel, out_shape=jax.ShapeDtypeStruct((VR, 1, FEAT // 2),...  99.2 us
    unnamed x1, local copies, waits for them, and re-layouts  4.29 us

profile of v2, /device:TPU:1, one launch (start us, length us, event | category | flops | bytes accessed | tf_op | source)
XLA Modules:
  0.0 103.5 jit_solution(17927016252672097343)
XLA Ops:
  0.0 99.2 %shard_map.64 = f32[502,1,1024]{2,1,0:T(1,128)} custom-call(s32[1,512]{1,0:T(1,128)} %ids_ref.1, f32[8,1,256]{2,1,0:T(1,128)} %bitcast.1, bf16[1,512,2048]{2,1,0:T(8,128)(2,1)} %emb_hbm.1, bf16[1,512,2048]{2,1,0:T(8,128)(2,1)} %pg_hbm.1, bf16[1,2048,2048]{2,1,0:T(8,128)(2,1)} %w_hbm.1, bf16[1,512,2048]{2,1,0:T(8,128)(2,1)} %st_hbm.1), custom_call_target="tpu_custom_call" | custom-call | tf_op jit(solution)/shard_map/pallas_call | solution.py:365
  99.2 4.3 %copy.8 = f32[502,1,1024]{2,1,0:T(1,128)} copy(f32[502,1,1024]{2,1,0:T(1,128)} %shard_map.64) | data formatting | bytes 4112384

commit v3 on v2

--- a/solution.py
+++ b/solution.py
@@ -21,6 +21,7 @@
 NB = FEAT // BF
 NF = FEAT // CF
 NC = NF // 2
+AHEAD = 4
 SLOTS = NDP * CAP
 ROWS = 2 * SLOTS
 HALF = VR // 2
@@ -58,7 +59,7 @@
     pg_hbm,
     w_hbm,
     st_hbm,
-    out_hbm,
+    table,
     pg,
     w,
     emb,
@@ -85,7 +86,6 @@
     near_rx,
     back_tx,
     back_rx,
-    table,
     in_sem,
     sum_sem,
     ids_sem,
@@ -97,7 +97,6 @@
     irsem,
     tab_ssem,
     tab_rsem,
-    osem,
 ):
     core = lax.axis_index("pipe")
     me = lax.axis_index("dp")
@@ -163,8 +162,6 @@
         device_id={"pipe": 1 - core},
         device_id_type=MESH,
     )
-    pl.semaphore_wait(barrier, 41)
-    ids_copy.start()
     pg_in.wait()
 
     def project(b, carry):
@@ -193,8 +190,10 @@
         device_id={"mp": 1 - half},
         device_id_type=MESH,
     )
+    pl.semaphore_wait(barrier, 41)
+    ids_copy.start()
+    sums_copy.start()
     ids_copy.wait()
-    sums_copy.start()
     place[1], other_rows = placement(ids_rx[...], CAP)
     isend[...] = (own_rows + other_rows).reshape(NDP, 1, 128)
     for f in range(NF):
@@ -231,9 +230,6 @@
         part = ref.at[pl.ds(0, REMOTE)]
         pltpu.make_async_copy(part, part, sem).wait()
 
-    for kind in range(2):
-        send_blocks(isend, irecv.at[kind], issem.at[kind], irsem.at[kind], 1 - 2 * kind)
-
     sums_copy.wait()
     total = sums_tx[...] + sums_rx[...]
     inverse = lax.rsqrt(total[0:1] / D + EPS)
@@ -297,9 +293,6 @@
     def back(c):
         return pass_on(back_tx, back_rx, c, 2, -direction(c))
 
-    def put(c):
-        return pltpu.make_async_copy(table.at[c], out_hbm.at[:, :, pl.ds(c * CF, CF)], osem.at[c])
-
     def first_sums(c):
         await_blocks(recv.at[c], rsem.at[c])
         far_tx[c] = summed(c, 0, 3).astype(BF16)
@@ -319,13 +312,15 @@
         own = own + back_rx[c].astype(F32)
         near(c).wait()
         own = own + near_rx[c].astype(F32)
-        table[c] = own[:VR].reshape(VR, 1, CF)
-        put(c).start()
-
-    AHEAD = 2
-    for c in range(AHEAD):
-        hand_over(c)
-    for c in range(AHEAD):
+        table[:, :, c * CF : (c + 1) * CF] = own[:VR].reshape(VR, 1, CF)
+
+    hand_over(0)
+    hand_over(1)
+    spread(0)
+    for kind in range(2):
+        send_blocks(isend, irecv.at[kind], issem.at[kind], irsem.at[kind], 1 - 2 * kind)
+    for c in range(1, AHEAD):
+        hand_over(c + 1)
         spread(c)
 
     slot = lax.broadcasted_iota(I32, (NDP, ROWS), 1)
@@ -340,8 +335,8 @@
         onehot[kind] = jnp.where(lax.broadcasted_iota(I32, (VP, ROWS), 0) == index, 1.0, 0.0).astype(BF16)
 
     for c in range(NC + 2):
-        if c + AHEAD < NC:
-            hand_over(c + AHEAD)
+        if c + AHEAD + 1 < NC:
+            hand_over(c + AHEAD + 1)
         if c < NC:
             first_sums(c)
         if c + AHEAD < NC:
@@ -355,18 +350,17 @@
         await_blocks(isend, issem.at[kind])
     for c in range(NC):
         await_blocks(send.at[c], ssem.at[c])
-        put(c).wait()
 
 
 def on_device(token_ids, embedded, norm_gain, proj_grad, proj_weight, stream_grad):
     anywhere = pl.BlockSpec(memory_space=pl.ANY)
     vmem = pl.BlockSpec(memory_space=pltpu.VMEM)
     dma = pltpu.SemaphoreType.DMA
-    return pl.pallas_call(
+    table = pl.pallas_call(
         kernel,
-        out_shape=jax.ShapeDtypeStruct((VR, 1, FEAT // 2), F32),
+        out_shape=pltpu.VMEM((VR, 1, FEAT // 2), F32),
         in_specs=[vmem, vmem] + [anywhere] * 4,
-        out_specs=anywhere,
+        out_specs=vmem,
         scratch_shapes=[
             pltpu.VMEM((TOK, INNER), BF16),
             pltpu.VMEM((NB, BF, INNER), BF16),
@@ -394,7 +388,6 @@
             pltpu.VMEM((NC, VP, CF), BF16),
             pltpu.VMEM((NC, VP, CF), BF16),
             pltpu.VMEM((NC, VP, CF), BF16),
-            pltpu.VMEM((NC, VR, 1, CF), F32),
             dma((1 + NB + 2 * NF,)),
             dma((2,)),
             dma((2,)),
@@ -406,10 +399,9 @@
             dma((2,)),
             dma((3, NC)),
             dma((3, NC)),
-            dma((NC,)),
         ],
         compiler_params=pltpu.CompilerParams(
-            collective_id=0, has_side_effects=True, vmem_limit_bytes=58 * 1024 * 1024
+            collective_id=0, has_side_effects=True, vmem_limit_bytes=56 * 1024 * 1024
         ),
     )(
         token_ids,
@@ -419,6 +411,7 @@
         proj_weight,
         stream_grad,
     )
+    return table
 
 
 def solution(mesh):

time: 106 us -> 94.2 us (0.89); the launches traced: 103 us -> 93.4 us
  Pallas kernels: 99.2 us -> 92.1 us
  local copies, waits for them, and re-layouts: 4.29 us -> 1.3 us
    pallas_call x1, Pallas kernels: 99.2 us -> 92.1 us  [on_device(): pl.pallas_call(kernel, out_shape=pltpu.VMEM((VR, 1, FEAT // 2), F32), in_...]
    unnamed x1, local copies, waits for them, and re-layouts: 4.29 us -> 1.3 us
where the time goes in v3:
time: 94.2 us; the launch traced here: 93.4 us
  Pallas kernels  92.1 us (98%)
  local copies, waits for them, and re-layouts  1.3 us (1%)
    pallas_call x1, Pallas kernels, on_device(): pl.pallas_call(kernel, out_shape=pltpu.VMEM((VR, 1, FEAT // 2), F32), in_...  92.1 us

profile of v3, /device:TPU:1, one launch (start us, length us, event | category | flops | bytes accessed | tf_op | source)
XLA Modules:
  0.0 93.4 jit_solution(3233683613839142313)
XLA Ops:
  0.0 92.1 %shard_map.64 = f32[502,1,1024]{2,1,0:T(1,128)S(1)} custom-call(s32[1,512]{1,0:T(1,128)} %ids_ref.1, f32[8,1,256]{2,1,0:T(1,128)} %bitcast.1, bf16[1,512,2048]{2,1,0:T(8,128)(2,1)} %emb_hbm.1, bf16[1,512,2048]{2,1,0:T(8,128)(2,1)} %pg_hbm.1, bf16[1,2048,2048]{2,1,0:T(8,128)(2,1)} %w_hbm.1, bf16[1,512,2048]{2,1,0:T(8,128)(2,1)} %st_hbm.1), custom_call_target="tpu_custom_call" | custom-call | tf_op jit(solution)/shard_map/pallas_call | solution.py:359
  92.1 1.3 %copy.8 = f32[502,1,1024]{2,1,0:T(1,128)} copy(f32[502,1,1024]{2,1,0:T(1,128)S(1)} %shard_map.64) | data formatting | bytes 4112384

commit v4 on v3

--- a/solution.py
+++ b/solution.py
@@ -17,7 +17,7 @@
 INNER = 2048
 FEAT = 2048
 CF = 128
-BF = 256
+BF = 512
 NB = FEAT // BF
 NF = FEAT // CF
 NC = NF // 2
@@ -145,8 +145,8 @@
     pg_in.start()
     for b in range(NB):
         w_in(b).start()
-        emb_in(2 * b).start()
-        emb_in(2 * b + 1).start()
+        for f in range(BF // CF * b, BF // CF * (b + 1)):
+            emb_in(f).start()
     for f in range(NF):
         st_in(f).start()
 
@@ -167,8 +167,8 @@
     def project(b, carry):
         in_copy(w_hbm.at[0, pl.ds(0, BF), :], w.at[b], 1 + b).wait()
         s = lax.dot_general(pg[...], w[b], NT, preferred_element_type=F32) * gain_ref[b]
-        for i in range(2):
-            f = 2 * b + i
+        for i in range(BF // CF):
+            f = BF // CF * b + i
             in_copy(emb_hbm.at[0, :, pl.ds(0, CF)], emb.at[f], 1 + NB + f).wait()
             part = s[:, i * CF : (i + 1) * CF]
             scaled[f] = part
@@ -302,15 +302,15 @@
 
     def second_sums(c):
         own = summed(c, 3, 1)
-        far(c).wait()
+        far(c).wait_recv()
         near_tx[c] = (own + far_rx[c].astype(F32)).astype(BF16)
         near(c).start()
 
     def last_sums(c):
         own = summed(c, 4, 1)
-        back(c).wait()
+        back(c).wait_recv()
         own = own + back_rx[c].astype(F32)
-        near(c).wait()
+        near(c).wait_recv()
         own = own + near_rx[c].astype(F32)
         table[:, :, c * CF : (c + 1) * CF] = own[:VR].reshape(VR, 1, CF)
 
@@ -350,6 +350,8 @@
         await_blocks(isend, issem.at[kind])
     for c in range(NC):
         await_blocks(send.at[c], ssem.at[c])
+        for copy in (far(c), near(c), back(c)):
+            copy.wait_send()
 
 
 def on_device(token_ids, embedded, norm_gain, proj_grad, proj_weight, stream_grad):

time: 94.2 us -> 93.8 us (level)
  no operation moved by 1% of the time
where the time goes in v4:
time: 93.8 us; the launch traced here: 93.1 us
  Pallas kernels  91.7 us (98%)
  local copies, waits for them, and re-layouts  1.3 us (1%)
    pallas_call x1, Pallas kernels, on_device(): pl.pallas_call(kernel, out_shape=pltpu.VMEM((VR, 1, FEAT // 2), F32), in_...  91.7 us

profile of v4, /device:TPU:1, one launch (start us, length us, event | category | flops | bytes accessed | tf_op | source)
XLA Modules:
  0.0 93.1 jit_solution(7419641557639966582)
XLA Ops:
  0.0 91.7 %shard_map.64 = f32[502,1,1024]{2,1,0:T(1,128)S(1)} custom-call(s32[1,512]{1,0:T(1,128)} %ids_ref.1, f32[4,1,512]{2,1,0:T(1,128)} %bitcast.1, bf16[1,512,2048]{2,1,0:T(8,128)(2,1)} %emb_hbm.1, bf16[1,512,2048]{2,1,0:T(8,128)(2,1)} %pg_hbm.1, bf16[1,2048,2048]{2,1,0:T(8,128)(2,1)} %w_hbm.1, bf16[1,512,2048]{2,1,0:T(8,128)(2,1)} %st_hbm.1), custom_call_target="tpu_custom_call" | custom-call | tf_op jit(solution)/shard_map/pallas_call | solution.py:361
  91.8 1.3 %copy.8 = f32[502,1,1024]{2,1,0:T(1,128)} copy(f32[502,1,1024]{2,1,0:T(1,128)S(1)} %shard_map.64) | data formatting | bytes 4112384

commit v5 on v4

--- a/solution.py
+++ b/solution.py
@@ -334,17 +334,17 @@
         index = jnp.sum(jnp.where(take, spots, 0.0), axis=0, keepdims=True).astype(I32) + HALF
         onehot[kind] = jnp.where(lax.broadcasted_iota(I32, (VP, ROWS), 0) == index, 1.0, 0.0).astype(BF16)
 
-    for c in range(NC + 2):
+    for c in range(NC + 3):
         if c + AHEAD + 1 < NC:
             hand_over(c + AHEAD + 1)
         if c < NC:
             first_sums(c)
         if c + AHEAD < NC:
             spread(c + AHEAD)
-        if 0 <= c - 1 < NC:
-            second_sums(c - 1)
         if 0 <= c - 2 < NC:
-            last_sums(c - 2)
+            second_sums(c - 2)
+        if 0 <= c - 3 < NC:
+            last_sums(c - 3)
 
     for kind in range(2):
         await_blocks(isend, issem.at[kind])

time: 93.8 us -> 93.7 us (level)
  no operation moved by 1% of the time
where the time goes in v5:
time: 93.7 us; the launch traced here: 93.6 us
  Pallas kernels  92.2 us (98%)
  local copies, waits for them, and re-layouts  1.3 us (1%)
    pallas_call x1, Pallas kernels, on_device(): pl.pallas_call(kernel, out_shape=pltpu.VMEM((VR, 1, FEAT // 2), F32), in_...  92.2 us

profile of v5, /device:TPU:1, one launch (start us, length us, event | category | flops | bytes accessed | tf_op | source)
XLA Modules:
  0.0 93.6 jit_solution(13994128250354144890)
XLA Ops:
  0.0 92.2 %shard_map.64 = f32[502,1,1024]{2,1,0:T(1,128)S(1)} custom-call(s32[1,512]{1,0:T(1,128)} %ids_ref.1, f32[4,1,512]{2,1,0:T(1,128)} %bitcast.1, bf16[1,512,2048]{2,1,0:T(8,128)(2,1)} %emb_hbm.1, bf16[1,512,2048]{2,1,0:T(8,128)(2,1)} %pg_hbm.1, bf16[1,2048,2048]{2,1,0:T(8,128)(2,1)} %w_hbm.1, bf16[1,512,2048]{2,1,0:T(8,128)(2,1)} %st_hbm.1), custom_call_target="tpu_custom_call" | custom-call | tf_op jit(solution)/shard_map/pallas_call | solution.py:361
  92.2 1.3 %copy.8 = f32[502,1,1024]{2,1,0:T(1,128)} copy(f32[502,1,1024]{2,1,0:T(1,128)S(1)} %shard_map.64) | data formatting | bytes 4112384
